TPU v7x, 32 devices: a whole 2x2x4 slice. The times are simulated.
32 devices in a mesh: grp: 2 (over x), tile: 16 (over z, y, core).
Axes of the slice: x: 2, y: 2, z: 4, core: 2. Of those that a mesh axis runs over, the one named last changes fastest.
Arguments:
- habitat: int32 [32, 4, 512], P(('grp', 'tile')), parts along dimension 0, may hold values from 0 to 15
- table: float32 [16], replicated, may hold values from 0.25 to 2
- source_cell: int32 [512], P('grp'), parts along dimension 0, may hold values from 0 to 32767
- ground_cell: int32 [512], P('grp'), parts along dimension 0, may hold values from 0 to 32767
- start_potential: float32 [32, 4, 512, 256], P(('grp', 'tile')), parts along dimension 0, may hold values from -30 to 30
Outputs:
- potentials: float32 [32, 4, 512, 256], P(('grp', 'tile')), parts along dimension 0
- residual: float32 [32, 4, 512, 256], P(('grp', 'tile')), parts along dimension 0
- resistance: float32 [512], P('grp'), parts along dimension 0
There are 2 independent parts, one for each index of `grp`. A program takes and returns all parts, laid end to end along the dimension named above; an argument that names none is the same for every part. Nothing has to cross between parts.
Inputs may be any that keep to these rules, and one draw needn't show every extreme that they name: `source_cell`: an index row * 1024 + column of the raster. `ground_cell`: an index row * 1024 + column of the raster.
All inputs are finite; a program needn't handle non-finite values.
Results may differ from a plain program's by a relative error of at most 0.00018.
Values sent between devices are 32-bit elements; how exact they have to be, the bound alone decides.
A program may use at most 128 MiB of HBM per device.

v0:
```python
import functools

import jax
import jax.numpy as jnp
from jax import lax
from jax.experimental import pallas as pl
from jax.experimental.pallas import tpu as pltpu
from jax.sharding import PartitionSpec as P

LANES = 128
TILE = 8
PAD = 2 * TILE
MESH = pl.DeviceIdType.MESH


def cuts(total, weights):
    bounds, seen = [0], 0
    for weight in weights:
        seen += weight
        bounds.append(total * seen // sum(weights))
    return bounds


def kernel(n, rows, cols, rounds, shared_weights, own_weights,
           table_hbm, habitat_hbm, source_hbm, ground_hbm, start_ref,
           pot_ref, res_ref, field_ref, coef_ref, drop_ref,
           X, R, W, U, V, H, D, C, T, TV, TH, S,
           table_ref, habitat_ref, source_ref, ground_ref, small_sem, load_sem,
           cond_recv, side_recv, edge_recv, cross_recv, shared_recv, relay_recv, near_recv, far_recv,
           sum_recv, cond_send, side_send, cross_send, near_send, far_send, relay_send, sum_send, hello):
    halves = X.shape[0]
    width = cols + 2 * PAD
    me = lax.axis_index("tile")
    chips = n // 2
    chip = me // 2
    core = me % 2
    odd = chip % 2
    side = me + 1 - 2 * core
    partner = me + 2 - 4 * odd
    diagonal = me - 2 + 4 * odd
    relay_to = me + 4 - 8 * odd
    relay_from = me - 4 + 8 * odd
    has_above = chip > 0
    has_below = chip < chips - 1
    has_diagonal = jnp.where(odd == 0, chip > 0, chip < chips - 1)
    can_relay = jnp.where(odd == 0, chip + 2 < chips, chip >= 2)
    gets_relay = jnp.where(odd == 0, chip >= 2, chip + 2 < chips)
    own = pl.ds(PAD, cols)
    body = cols // TILE - 1
    shared_at = cuts(body, shared_weights)
    own_at = [cuts(body, weights) for weights in own_weights]

    def remote(src, dst, send, recv, target):
        return pltpu.make_async_remote_copy(
            src_ref=src, dst_ref=dst, send_sem=send, recv_sem=recv,
            device_id={"tile": target}, device_id_type=MESH)

    def arrived(place, recv):
        remote(place, place, near_send.at[0], recv, partner).wait_recv()

    def drained(place, send):
        remote(place, place, send, sum_recv.at[0], partner).wait_send()

    def signal(sem, target):
        pl.semaphore_signal(sem, inc=1, device_id={"tile": target}, device_id_type=MESH)

    def load(h):
        return pltpu.make_async_copy(
            start_ref.at[0, :, :, pl.ds(h * LANES, LANES)], X.at[h, pl.ds(rows, rows), own, :],
            load_sem.at[h])

    smalls = [
        pltpu.make_async_copy(src, dst, small_sem.at[k])
        for k, (src, dst) in enumerate((
            (table_hbm, table_ref), (habitat_hbm, habitat_ref),
            (source_hbm, source_ref), (ground_hbm, ground_ref)))
    ]

    barrier = pltpu.get_barrier_semaphore()
    signal(barrier, side)

    @pl.when(has_above)
    def _():
        signal(barrier, me - 2)
        signal(barrier, side - 2)

    @pl.when(has_below)
    def _():
        signal(barrier, me + 2)
        signal(barrier, side + 2)

    @pl.when(gets_relay)
    def _():
        signal(barrier, relay_from)

    for h in range(halves):
        load(h).start()
    for copy in smalls:
        copy.start()

    inner = pl.multiple_of(PAD + (1 - core) * (cols - TILE), TILE)
    outer = pl.multiple_of((1 - core) * TILE + core * (PAD + cols), TILE)
    halo = pl.multiple_of(core * TILE + (1 - core) * (PAD + cols), TILE)
    inner_at, outer_at, halo_at = pl.ds(inner, TILE), pl.ds(outer, TILE), pl.ds(halo, TILE)

    def span(bounds, j):
        start = pl.multiple_of(PAD + core * TILE + bounds[j] * TILE, TILE)
        return pl.ds(start, (bounds[j + 1] - bounds[j]) * TILE)

    def side_copy(h):
        place = pl.ds(rows, rows)
        return remote(X.at[h, place, inner_at, :], X.at[h, place, outer_at, :],
                      side_send.at[0], side_recv.at[h], side)

    def side_wait(h):
        arrived(X.at[h, pl.ds(rows, rows), halo_at, :], side_recv.at[h])

    def edge_near(h):
        return remote(X.at[h, pl.ds(rows + 1 - odd, rows - 1), inner_at, :],
                      X.at[h, pl.ds(odd * 2 * rows + 1 - odd, rows - 1), inner_at, :],
                      near_send.at[0], edge_recv.at[h, 0], partner)

    def edge_far(h):
        return remote(X.at[h, pl.ds(rows + odd, rows - 1), inner_at, :],
                      X.at[h, pl.ds((1 - odd) * 2 * rows + odd, rows - 1), inner_at, :],
                      far_send.at[0], edge_recv.at[h, 1], diagonal)

    near_rows = pl.ds((1 - odd) * 2 * rows + odd, rows - 1)
    far_rows = pl.ds(odd * 2 * rows + 1 - odd, rows - 1)

    def cross(h, k):
        place = (near_rows, far_rows)[k]
        return remote(X.at[h, place, inner_at, :], X.at[h, place, outer_at, :],
                      cross_send.at[k], cross_recv.at[h, k], side)

    def cross_wait(h, k):
        arrived(X.at[h, (near_rows, far_rows)[k], halo_at, :], cross_recv.at[h, k])

    def shared_copy(h, j):
        at = span(shared_at, j)
        return remote(X.at[h, pl.ds(rows + 1, rows - 2), at, :],
                      X.at[h, pl.ds(odd * 2 * rows + 1, rows - 2), at, :],
                      near_send.at[0], shared_recv.at[h, j], partner)

    def relay_copy(h, j):
        at = span(shared_at, j)
        return remote(X.at[h, pl.ds((1 - odd) * 2 * rows + 1, rows - 2), at, :],
                      X.at[h, pl.ds(odd * 2 * rows + 1, rows - 2), at, :],
                      relay_send.at[0], relay_recv.at[h, j], relay_to)

    def near_copy(h, k):
        at = span(own_at[h], k)
        row = (1 - odd) * (rows - 1)
        return remote(X.at[h, rows + row, at, :], X.at[h, odd * 2 * rows + row, at, :],
                      near_send.at[0], near_recv.at[h, k], partner)

    def far_copy(h, k):
        at = span(own_at[h], k)
        row = odd * (rows - 1)
        return remote(X.at[h, rows + row, at, :], X.at[h, (1 - odd) * 2 * rows + row, at, :],
                      far_send.at[0], far_recv.at[h, k], diagonal)

    pl.semaphore_wait(
        barrier,
        1 + 2 * has_above.astype(jnp.int32) + 2 * has_below.astype(jnp.int32) + can_relay.astype(jnp.int32))

    for h in range(halves):
        load(h).wait()
        side_copy(h).start()
        edge_near(h).start()

        @pl.when(has_diagonal)
        def _():
            edge_far(h).start()

    for h in range(halves):
        for j in range(len(shared_weights)):
            shared_copy(h, j).start()
        for k in range(len(own_weights[h])):
            @pl.when(has_diagonal)
            def _():
                far_copy(h, k).start()
            near_copy(h, k).start()

    for copy in smalls:
        copy.wait()
    cells = habitat_ref[0]
    cond = jnp.zeros(cells.shape, jnp.float32)
    for level in range(table_ref.shape[0]):
        cond = jnp.where(cells == level, table_ref[level], cond)
    C[5, 0:rows, :] = cond
    C[5, rows:2 * rows, :] = cond

    def cond_copy(target, slot, kind):
        return remote(C.at[5], C.at[slot], cond_send.at[kind], cond_recv.at[slot], target)

    cond_copy(side, 2, 0).start()

    @pl.when(has_above)
    def _():
        cond_copy(me - 2, 1, 1).start()
        cond_copy(side - 2, 4, 1).start()

    @pl.when(has_below)
    def _():
        cond_copy(me + 2, 0, 2).start()
        cond_copy(side + 2, 3, 2).start()

    def zero(ref, h, c):
        ref[h, :, c:c + TILE, :] = jnp.zeros((ref.shape[1], TILE, LANES), jnp.float32)

    for h in range(halves):
        for c in (0, width - TILE):
            zero(X, h, c)
            zero(R, h, c)
            zero(W, h, c)

        @pl.when(core == 0)
        def _():
            zero(X, h, TILE)

        @pl.when(core == 1)
        def _():
            zero(X, h, width - PAD)

        @pl.when(jnp.logical_not(has_above))
        def _():
            X[h, 0:rows] = jnp.zeros((rows, width, LANES), jnp.float32)

        @pl.when(jnp.logical_not(has_below))
        def _():
            X[h, 2 * rows:3 * rows] = jnp.zeros((rows, width, LANES), jnp.float32)

    for h in range(halves):
        arrived(X.at[h, near_rows, inner_at, :], edge_recv.at[h, 0])
        cross(h, 0).start()

    @pl.when(has_diagonal)
    def _():
        for h in range(halves):
            arrived(X.at[h, far_rows, inner_at, :], edge_recv.at[h, 1])
            cross(h, 1).start()

    arrived(C.at[2], cond_recv.at[2])

    @pl.when(has_above)
    def _():
        arrived(C.at[0], cond_recv.at[0])
        arrived(C.at[3], cond_recv.at[3])

    @pl.when(has_below)
    def _():
        arrived(C.at[1], cond_recv.at[1])
        arrived(C.at[4], cond_recv.at[4])

    @pl.when(jnp.logical_not(has_above))
    def _():
        for slot in (0, 3):
            C[slot] = jnp.zeros(C.shape[1:], jnp.float32)

    @pl.when(jnp.logical_not(has_below))
    def _():
        for slot in (1, 4):
            C[slot] = jnp.zeros(C.shape[1:], jnp.float32)

    def greet(r):
        d = 2 << r

        @pl.when(me >= d)
        def _():
            signal(hello.at[r], me - d)

        @pl.when(me + d < n)
        def _():
            signal(hello.at[r], me + d)

    def greeted(r):
        d = 2 << r
        pl.semaphore_wait(hello.at[r], (me >= d).astype(jnp.int32) + (me + d < n).astype(jnp.int32))

    greet(0)

    first = lax.broadcasted_iota(jnp.int32, (2 * rows, LANES), 0) < rows

    def turned(above, here, below, j):
        lanes = slice(j * LANES, (j + 1) * LANES)
        top = jnp.where(first, C[above, :, lanes], C[here, :, lanes])
        blank = jnp.zeros((LANES - 4 * rows, LANES), jnp.float32)
        return jnp.transpose(jnp.concatenate([top, C[below, :, lanes], blank], 0))

    for j in range(cols // LANES):
        T[PAD + j * LANES:PAD + (j + 1) * LANES, :] = turned(0, 5, 1, j)
    for c in (0, TILE, width - PAD, width - TILE):
        T[c:c + TILE, :] = jnp.zeros((TILE, LANES), jnp.float32)

    @pl.when(core == 0)
    def _():
        T[width - PAD:width - TILE, :] = turned(3, 2, 4, 0)[0:TILE]

    @pl.when(core == 1)
    def _():
        T[TILE:PAD, :] = turned(3, 2, 4, cols // LANES - 1)[LANES - TILE:]

    def global_col(c):
        return core * cols - PAD + c + lax.broadcasted_iota(jnp.int32, (TILE, LANES), 0)

    global_row = chip * rows - rows + lax.broadcasted_iota(jnp.int32, (TILE, LANES), 1)
    total_rows, total_cols = chips * rows, 2 * cols

    def edges(t, _):
        c = pl.multiple_of(t * TILE, TILE)
        here = T[pl.ds(c, TILE), :]
        east = T[pl.ds(c + 1, TILE), :]
        south = pltpu.roll(here, LANES - 1, 1)
        gc = global_col(c)
        in_row = (global_row >= 0) & (global_row < total_rows - 1)
        TV[pl.ds(c, TILE), :] = jnp.where(in_row, 0.5 * (here + south), 0.0)
        in_col = (gc >= 0) & (gc < total_cols - 1)
        TH[pl.ds(c, TILE), :] = jnp.where(in_col, 0.5 * (here + east), 0.0)
        return 0

    TH[0:TILE, :] = jnp.zeros((TILE, LANES), jnp.float32)
    H[:, 0:TILE, :] = jnp.zeros((H.shape[0], TILE, LANES), jnp.float32)
    lax.fori_loop(1, width // TILE - 1, edges, 0, unroll=2)

    def spread(t, _):
        c = pl.multiple_of(t * TILE, TILE)
        at = pl.ds(c, TILE)
        v = TV[at, :]
        east = TH[at, :]
        west = TH[pl.ds(c - 1, TILE), :]
        diag = v + pltpu.roll(v, 1, 1) + east + west
        shape = (TILE, LANES)
        for k in range(2 * rows + 1):
            V[k, at, :] = jnp.broadcast_to(v[:, k + 1:k + 2], shape)
        for k in range(2 * rows):
            H[k, at, :] = jnp.broadcast_to(east[:, k + 2:k + 3], shape)
            D[k, at, :] = jnp.broadcast_to(diag[:, k + 2:k + 3], shape)
        return 0

    tiles = width // TILE

    def relay(h, j):
        arrived(X.at[h, pl.ds((1 - odd) * 2 * rows + 1, rows - 2), span(shared_at, j), :],
                shared_recv.at[h, j])

        @pl.when(can_relay)
        def _():
            relay_copy(h, j).start()

    parts = len(shared_weights)
    splits = cuts(tiles - 2, [1] * parts)
    for j in range(parts):
        lax.fori_loop(1 + splits[j], 1 + splits[j + 1], spread, 0)
        relay(0, j)
        if j < rounds:
            greeted(j)
            if j + 1 < rounds:
                greet(j + 1)
    for r in range(parts, rounds):
        greeted(r)
        if r + 1 < rounds:
            greet(r + 1)

    def ends(h, lag, first, end):
        return [first] + [PAD // TILE + core + bound - lag for bound in own_at[h][1:-1]] + [end]

    def shape_of(cells, h, top):
        base = (chip * rows + top) * total_cols + core * cols - PAD
        return jnp.broadcast_to(cells[h:h + 1, :] - base, (TILE, LANES))

    def applied(ref, h, skip, count, c, low, grounds):
        at = pl.ds(c, TILE)
        west = pl.ds(c - 1, TILE)
        east = pl.ds(c + 1, TILE)
        column = c + lax.broadcasted_iota(jnp.int32, (TILE, LANES), 0)
        mid = ref[h, skip + 1, at, :]
        flow = V[low, at, :] * ref[h, skip, at, :]
        for k in range(count):
            after = ref[h, skip + k + 2, at, :]
            v = V[low + k + 1, at, :]
            grounded = column == grounds[k]
            diag = D[low + k, at, :]
            out = jnp.where(grounded, diag + 1.0, diag) * mid - flow
            out = out - v * after
            out = out - H[low + k, west, :] * ref[h, skip + 1 + k, west, :]
            out = out - H[low + k, at, :] * ref[h, skip + 1 + k, east, :]
            yield k, out, mid, grounded, column
            flow = v * mid
            mid = after

    def zeros():
        return tuple(jnp.zeros((TILE, LANES), jnp.float32) for _ in range(7))

    def compute(h, j, acc):
        def named(cells, top, count):
            return [shape_of(cells, h, top + k) for k in range(count)]

        count_r, count_w = 2 * rows, 2 * rows - 2
        src_r, gnd_r = named(source_ref, -2, count_r), named(ground_ref, -2, count_r)
        gnd_w = named(ground_ref, -1, count_w)
        src_u, gnd_u = named(source_ref, 0, rows), named(ground_ref, 0, rows)

        def pass_r(t, _):
            c = pl.multiple_of(t * TILE, TILE)
            for k, a, _mid, _g, column in applied(X, h, 1, count_r, c, 0, gnd_r):
                R[h, k, pl.ds(c, TILE), :] = jnp.where(column == src_r[k], 1.0 - a, -a)
            return 0

        def pass_w(t, _):
            c = pl.multiple_of(t * TILE, TILE)
            for k, a, _mid, _g, _column in applied(R, h, 0, count_w, c, 1, gnd_w):
                W[h, k, pl.ds(c, TILE), :] = a
            return 0

        def pass_u(t, acc):
            c = pl.multiple_of(t * TILE, TILE)
            at = pl.ds(c, TILE)
            to = pl.ds(c - PAD, TILE)
            for k, u, w, grounded, column in applied(W, h, 0, rows, c, 2, gnd_u):
                r = R[h, 2 + k, at, :]
                x = X[h, rows + k, at, :]
                if h < halves - 1:
                    U[h, k, to, :] = u
                else:
                    for place, value in enumerate((x, r, w, u)):
                        field_ref[place, k, to, :] = value
                sign = jnp.where(column == src_u[k], 1.0, 0.0) - jnp.where(grounded, 1.0, 0.0)
                terms = (r * r, r * w, w * w, w * u, sign * x, sign * r, sign * w)
                acc = tuple(s + term for s, term in zip(acc, terms))
            return acc

        r_ends, w_ends, u_ends = (
            ends(h, lag, 1 + (lag == 3), tiles - 1 - (lag == 3)) for lag in (1, 2, 3))
        lax.fori_loop(r_ends[j], r_ends[j + 1], pass_r, 0)
        lax.fori_loop(w_ends[j], w_ends[j + 1], pass_w, 0)
        return lax.fori_loop(u_ends[j], u_ends[j + 1], pass_u, acc)

    def sum_copy(h, d):
        return remote(S.at[h, me], S.at[h, me], sum_send.at[0], sum_recv.at[h], (me + d) % n)

    def send_sums(h, acc):
        sums = [jnp.sum(s, axis=0, keepdims=True) for s in acc]
        S[h, me] = jnp.concatenate(sums + [jnp.zeros((1, LANES), jnp.float32)], 0)
        lax.fori_loop(1, n, lambda d, _: (sum_copy(h, d).start(), 0)[1], 0)

    def totals(h):
        arrived(S.at[h, pl.ds(0, n - 1)], sum_recv.at[h])
        total = S[h, 0]
        for k in range(1, n):
            total = total + S[h, k]
        m0, m1, m2, m3, ex, er, ew = (total[k:k + 1] for k in range(7))
        a0 = m0 / m1
        next_norm = a0 * (a0 * m2 - m1)
        ratio = next_norm / m0
        curve = m1 - a0 * (2.0 * m2 - a0 * m3)
        a1 = next_norm / (curve - ratio * next_norm / a0)
        p = a0 + a1 * (1.0 + ratio)
        q = a1 * a0
        drop_ref[h:h + 1, :] = ex + p * er - q * ew
        return p, q

    def finish(h):
        p, q = totals(h)
        p1 = jnp.broadcast_to(p, (TILE, LANES))
        q1 = jnp.broadcast_to(q, (TILE, LANES))

        def last(t, _):
            c = pl.multiple_of(t * TILE, TILE)
            at = pl.ds(c + PAD, TILE)
            to = pl.ds(c, TILE)
            for k in range(rows):
                r = R[h, 2 + k, at, :]
                w = W[h, 1 + k, at, :]
                pot_ref[h, k, to, :] = X[h, rows + k, at, :] + p1 * r - q1 * w
                res_ref[h, k, to, :] = r - p1 * w + q1 * U[h, k, to, :]
            return 0

        lax.fori_loop(0, cols // TILE, last, 0)

    for h in range(halves):
        side_wait(h)
        cross_wait(h, 0)

        @pl.when(has_diagonal)
        def _():
            cross_wait(h, 1)

        acc = zeros()
        relayed = 0
        for k in range(len(own_weights[h])):
            while relayed < parts and shared_at[relayed] < own_at[h][k + 1]:
                @pl.when(gets_relay)
                def _():
                    arrived(X.at[h, pl.ds(odd * 2 * rows + 1, rows - 2), span(shared_at, relayed), :],
                            relay_recv.at[h, relayed])
                relayed += 1

            @pl.when(has_diagonal)
            def _():
                arrived(X.at[h, odd * 2 * rows + (1 - odd) * (rows - 1), span(own_at[h], k), :],
                        far_recv.at[h, k])
            arrived(X.at[h, (1 - odd) * 2 * rows + odd * (rows - 1), span(own_at[h], k), :],
                    near_recv.at[h, k])
            acc = compute(h, k, acc)
        send_sums(h, acc)
        if h < halves - 1:
            for j in range(parts):
                relay(h + 1, j)
                if j == parts // 2 - 1:
                    finish(h)

    p, q = totals(halves - 1)
    coef_ref[...] = jnp.concatenate([p, q, jnp.zeros((TILE - 2, LANES), jnp.float32)], 0)

    drained(C.at[0], cond_send.at[0])

    @pl.when(has_above)
    def _():
        drained(C.at[pl.ds(0, 2)], cond_send.at[1])

    @pl.when(has_below)
    def _():
        drained(C.at[pl.ds(0, 2)], cond_send.at[2])

    drained(X.at[:, pl.ds(0, rows), pl.ds(0, TILE), :], side_send.at[0])
    drained(X.at[:, pl.ds(0, rows - 1), pl.ds(0, TILE), :], cross_send.at[0])
    drained(X.at[:, pl.ds(0, rows - 1), pl.ds(0, cols), :], near_send.at[0])

    @pl.when(has_diagonal)
    def _():
        drained(X.at[:, pl.ds(0, rows - 1), pl.ds(0, TILE), :], cross_send.at[1])
        drained(X.at[:, pl.ds(0, 1), pl.ds(0, cols + (rows - 2) * TILE), :], far_send.at[0])

    @pl.when(can_relay)
    def _():
        drained(X.at[:, pl.ds(0, rows - 2), pl.ds(0, cols - TILE), :], relay_send.at[0])

    drained(S.at[:, pl.ds(0, n - 1)], sum_send.at[0])


def closing(pot_ref, res_ref, field_ref, coef_ref, drop_ref, pot_out, res_out, drop_out,
            P1, Q1, sem):
    rows, cols = field_ref.shape[1], field_ref.shape[2]
    before = pot_ref.shape[0]

    def put(ref, out, h, c, count, k):
        return pltpu.make_async_copy(
            ref.at[:, pl.ds(c, count), :],
            out.at[0, :, pl.ds(c, count), pl.ds(h * LANES, LANES)], sem.at[k])

    for h in range(before):
        put(pot_ref.at[h], pot_out, h, 0, cols, 0).start()
        put(res_ref.at[h], res_out, h, 0, cols, 1).start()
    drop = pltpu.make_async_copy(drop_ref, drop_out, sem.at[2])
    drop.start()

    p1 = jnp.broadcast_to(coef_ref[0:1, :], (TILE, LANES))
    q1 = jnp.broadcast_to(coef_ref[1:2, :], (TILE, LANES))
    pieces = 4
    step = cols // pieces

    def last(t, _):
        c = pl.multiple_of(t * TILE, TILE)
        at = pl.ds(c, TILE)
        for k in range(rows):
            x, r, w, u = (field_ref[place, k, at, :] for place in range(4))
            P1[k, at, :] = x + p1 * r - q1 * w
            Q1[k, at, :] = r - p1 * w + q1 * u
        return 0

    for piece in range(pieces):
        lax.fori_loop(piece * step // TILE, (piece + 1) * step // TILE, last, 0, unroll=2)
        put(P1, pot_out, before, piece * step, step, 0).start()
        put(Q1, res_out, before, piece * step, step, 1).start()

    for k, out in enumerate((pot_out, res_out)):
        pltpu.make_async_copy(out, out, sem.at[k]).wait()
    drop.wait()


def solution(mesh):
    n = mesh.shape["tile"]
    rounds = max(1, (n // 2 - 1).bit_length())

    def shards(habitat, table, source_cell, ground_cell, start_potential):
        _, rows, cols, rhs = start_potential.shape
        halves = rhs // LANES
        width = cols + 2 * PAD
        f32 = jnp.float32
        dma = pltpu.SemaphoreType.DMA
        field = jax.ShapeDtypeStruct(start_potential.shape, f32)
        part = jax.ShapeDtypeStruct((halves - 1, rows, cols, LANES), f32)
        drops = jax.ShapeDtypeStruct((halves, LANES), f32)
        vmem = pl.BlockSpec(memory_space=pltpu.VMEM)
        hbm = pl.BlockSpec(memory_space=pltpu.HBM)
        shared_weights = (16, 16, 16, 15)
        own_weights = ((16, 16, 16, 15),) * (halves - 1) + ((9, 9, 9, 9, 9, 8, 6, 4),)
        parts, most = len(shared_weights), max(map(len, own_weights))
        stages = pl.pallas_call(
            functools.partial(kernel, n, rows, cols, rounds, shared_weights, own_weights),
            out_shape=(part, part, jax.ShapeDtypeStruct((4, rows, cols, LANES), f32),
                       jax.ShapeDtypeStruct((TILE, LANES), f32), drops),
            in_specs=[hbm] * 5,
            out_specs=(vmem,) * 5,
            scratch_shapes=[
                pltpu.VMEM((halves, 3 * rows, width, LANES), f32),
                pltpu.VMEM((halves, 2 * rows, width, LANES), f32),
                pltpu.VMEM((halves, 2 * rows - 2, width, LANES), f32),
                pltpu.VMEM((halves - 1, rows, cols, LANES), f32),
                pltpu.VMEM((2 * rows + 1, width, LANES), f32),
                pltpu.VMEM((2 * rows, width, LANES), f32),
                pltpu.VMEM((2 * rows, width, LANES), f32),
                pltpu.VMEM((6, 2 * rows, cols), f32),
                pltpu.VMEM((width, LANES), f32),
                pltpu.VMEM((width, LANES), f32),
                pltpu.VMEM((width, LANES), f32),
                pltpu.VMEM((halves, n, TILE, LANES), f32),
                pltpu.SMEM(table.shape, f32),
                pltpu.VMEM(habitat.shape, jnp.int32),
                pltpu.VMEM((halves, LANES), jnp.int32),
                pltpu.VMEM((halves, LANES), jnp.int32),
                dma((4,)), dma((halves,)),
                dma((5,)), dma((halves,)), dma((halves, 2)), dma((halves, 2)),
                dma((halves, parts)), dma((halves, parts)),
                dma((halves, most)), dma((halves, most)),
                dma((halves,)), dma((3,)), dma((1,)), dma((2,)),
                dma((1,)), dma((1,)), dma((1,)), dma((1,)),
                pltpu.SemaphoreType.REGULAR((rounds,)),
            ],
            compiler_params=pltpu.CompilerParams(
                collective_id=0, has_side_effects=True, vmem_limit_bytes=32 * 2**20),
        )(*(pltpu.with_memory_space_constraint(value, pltpu.HBM) for value in (
            table, habitat, source_cell.reshape(halves, LANES),
            ground_cell.reshape(halves, LANES), start_potential)))
        potentials, residual, drop = pl.pallas_call(
            closing,
            out_shape=(field, field, drops),
            in_specs=[vmem] * 5,
            out_specs=(hbm,) * 3,
            scratch_shapes=[
                pltpu.VMEM((rows, cols, LANES), f32),
                pltpu.VMEM((rows, cols, LANES), f32),
                dma((3,)),
            ],
            compiler_params=pltpu.CompilerParams(vmem_limit_bytes=16 * 2**20),
        )(*stages)
        return potentials, residual, drop.reshape(rhs)

    placed = (
        P(("grp", "tile"), None, None),
        P(),
        P("grp"),
        P("grp"),
        P(("grp", "tile"), None, None, None),
    )
    return jax.shard_map(
        shards,
        mesh=mesh,
        in_specs=placed,
        out_specs=(placed[4], placed[4], P("grp")),
        check_vma=False,
    )
```

profile of v0, /device:TPU:0, one launch (start us, length us, event | category | flops | bytes accessed | tf_op | source)
XLA Modules:
  0.0 95.3 jit_solution(11456205265948842275)
XLA Ops:
  0.6 92.6 %shard_map.76 = (f32[1,4,512,128]{3,2,1,0:T(8,128)S(1)}, f32[1,4,512,128]{3,2,1,0:T(8,128)S(1)}, f32[4,4,512,128]{3,2,1,0:T(8,128)S(1)}, f32[8,128]{1,0:T(8,128)S(1)}, f32[2,128]{1,0:T(2,128)S(1)}) custom-call(f32[16]{0:T(128)} %table_hbm.1, s32[1,4,512]{2,1,0:T(4,128)} %habitat_hbm.1, s32[2,128]{1,0:T(2,128)} %bitcast.3, s32[2,128]{1,0:T(2,128)} %bitcast.4, ...), custom_call_target="tpu_custom_call" | custom-call | tf_op jit(solution)/shard_map/pallas_call | solution.py:600
  93.2 2.0 %shard_map.77 = (f32[1,4,512,256]{3,2,1,0:T(8,128)}, f32[1,4,512,256]{3,2,1,0:T(8,128)}, f32[2,128]{1,0:T(2,128)}) custom-call(f32[1,4,512,128]{3,2,1,0:T(8,128)S(1)} %get-tuple-element.11.pot_ref, f32[1,4,512,128]{3,2,1,0:T(8,128)S(1)} %get-tuple-element.12.res_ref, f32[4,4,512,128]{3,2,1,0:T(8,128)S(1)} %get-tuple-element.13.field_ref, ...), custom_call_target="tpu_custom_call" | custom-call | tf_op jit(solution)/shard_map/pallas_call | solution.py:636
where the time goes:
time: 95.4 us; the launch traced here: 95.3 us
  Pallas kernels  94.6 us (99%)
    pallas_call x1, Pallas kernels, shards(): pl.pallas_call(functools.partial(kernel, n, rows, cols, rounds, shared_we...  92.6 us
    pallas_call x1, Pallas kernels, shards(): pl.pallas_call(closing, out_shape=(field, field, drops), in_specs=[vmem]...  2.03 us

commit v1 on v0

--- a/solution.py
+++ b/solution.py
@@ -21,13 +21,13 @@
     return bounds
 
 
-def kernel(n, rows, cols, rounds, shared_weights, own_weights,
+def kernel(n, rows, cols, rounds, ahead, pass_weights, own_weights,
            table_hbm, habitat_hbm, source_hbm, ground_hbm, start_ref,
            pot_ref, res_ref, field_ref, coef_ref, drop_ref,
            X, R, W, U, V, H, D, C, T, TV, TH, S,
            table_ref, habitat_ref, source_ref, ground_ref, small_sem, load_sem,
-           cond_recv, side_recv, edge_recv, cross_recv, shared_recv, relay_recv, near_recv, far_recv,
-           sum_recv, cond_send, side_send, cross_send, near_send, far_send, relay_send, sum_send, hello):
+           cond_recv, side_recv, edge_recv, cross_recv, pass_recv, relay_recv, near_recv,
+           sum_recv, cond_send, side_send, cross_send, near_send, edge_send, far_send, relay_send, sum_send, hello):
     halves = X.shape[0]
     width = cols + 2 * PAD
     me = lax.axis_index("tile")
@@ -47,7 +47,9 @@
     gets_relay = jnp.where(odd == 0, chip >= 2, chip + 2 < chips)
     own = pl.ds(PAD, cols)
     body = cols // TILE - 1
-    shared_at = cuts(body, shared_weights)
+    pass_at = [cuts(body, weights) for weights in pass_weights]
+    pass_sem = cuts(sum(map(len, pass_weights)), list(map(len, pass_weights)))
+    own_sem = cuts(sum(map(len, own_weights)), list(map(len, own_weights)))
     own_at = [cuts(body, weights) for weights in own_weights]
 
     def remote(src, dst, send, recv, target):
@@ -118,7 +120,7 @@
     def edge_near(h):
         return remote(X.at[h, pl.ds(rows + 1 - odd, rows - 1), inner_at, :],
                       X.at[h, pl.ds(odd * 2 * rows + 1 - odd, rows - 1), inner_at, :],
-                      near_send.at[0], edge_recv.at[h, 0], partner)
+                      edge_send.at[0], edge_recv.at[h, 0], partner)
 
     def edge_far(h):
         return remote(X.at[h, pl.ds(rows + odd, rows - 1), inner_at, :],
@@ -136,51 +138,23 @@
     def cross_wait(h, k):
         arrived(X.at[h, (near_rows, far_rows)[k], halo_at, :], cross_recv.at[h, k])
 
-    def shared_copy(h, j):
-        at = span(shared_at, j)
-        return remote(X.at[h, pl.ds(rows + 1, rows - 2), at, :],
-                      X.at[h, pl.ds(odd * 2 * rows + 1, rows - 2), at, :],
-                      near_send.at[0], shared_recv.at[h, j], partner)
+    def pass_copy(h, j):
+        at = span(pass_at[h], j)
+        return remote(X.at[h, pl.ds(rows + odd, rows - 1), at, :],
+                      X.at[h, pl.ds(odd * 2 * rows + odd, rows - 1), at, :],
+                      near_send.at[0], pass_recv.at[pass_sem[h] + j], partner)
 
     def relay_copy(h, j):
-        at = span(shared_at, j)
-        return remote(X.at[h, pl.ds((1 - odd) * 2 * rows + 1, rows - 2), at, :],
-                      X.at[h, pl.ds(odd * 2 * rows + 1, rows - 2), at, :],
-                      relay_send.at[0], relay_recv.at[h, j], relay_to)
+        at = span(pass_at[h], j)
+        return remote(X.at[h, pl.ds((1 - odd) * (2 * rows + 1), rows - 1), at, :],
+                      X.at[h, far_rows, at, :],
+                      relay_send.at[0], relay_recv.at[pass_sem[h] + j], relay_to)
 
     def near_copy(h, k):
         at = span(own_at[h], k)
         row = (1 - odd) * (rows - 1)
         return remote(X.at[h, rows + row, at, :], X.at[h, odd * 2 * rows + row, at, :],
-                      near_send.at[0], near_recv.at[h, k], partner)
-
-    def far_copy(h, k):
-        at = span(own_at[h], k)
-        row = odd * (rows - 1)
-        return remote(X.at[h, rows + row, at, :], X.at[h, (1 - odd) * 2 * rows + row, at, :],
-                      far_send.at[0], far_recv.at[h, k], diagonal)
-
-    pl.semaphore_wait(
-        barrier,
-        1 + 2 * has_above.astype(jnp.int32) + 2 * has_below.astype(jnp.int32) + can_relay.astype(jnp.int32))
-
-    for h in range(halves):
-        load(h).wait()
-        side_copy(h).start()
-        edge_near(h).start()
-
-        @pl.when(has_diagonal)
-        def _():
-            edge_far(h).start()
-
-    for h in range(halves):
-        for j in range(len(shared_weights)):
-            shared_copy(h, j).start()
-        for k in range(len(own_weights[h])):
-            @pl.when(has_diagonal)
-            def _():
-                far_copy(h, k).start()
-            near_copy(h, k).start()
+                      near_send.at[0], near_recv.at[own_sem[h] + k], partner)
 
     for copy in smalls:
         copy.wait()
@@ -191,20 +165,51 @@
     C[5, 0:rows, :] = cond
     C[5, rows:2 * rows, :] = cond
 
+    pl.semaphore_wait(
+        barrier,
+        1 + 2 * has_above.astype(jnp.int32) + 2 * has_below.astype(jnp.int32) + can_relay.astype(jnp.int32))
+
     def cond_copy(target, slot, kind):
         return remote(C.at[5], C.at[slot], cond_send.at[kind], cond_recv.at[slot], target)
 
+    def inner_lanes(which):
+        return pl.ds(pl.multiple_of(which * (cols - LANES), LANES), LANES)
+
+    def corner_copy(target, slot, kind):
+        at = inner_lanes(1 - core)
+        return remote(C.at[5, :, at], C.at[slot, :, at], cond_send.at[kind], cond_recv.at[slot], target)
+
+    def corner_wait(slot):
+        arrived(C.at[slot, :, inner_lanes(core)], cond_recv.at[slot])
+
     cond_copy(side, 2, 0).start()
 
     @pl.when(has_above)
     def _():
         cond_copy(me - 2, 1, 1).start()
-        cond_copy(side - 2, 4, 1).start()
+        corner_copy(side - 2, 4, 3).start()
 
     @pl.when(has_below)
     def _():
         cond_copy(me + 2, 0, 2).start()
-        cond_copy(side + 2, 3, 2).start()
+        corner_copy(side + 2, 3, 4).start()
+
+    for h in range(halves):
+        load(h).wait()
+        side_copy(h).start()
+        edge_near(h).start()
+
+        @pl.when(has_diagonal)
+        def _():
+            edge_far(h).start()
+
+    parts = list(map(len, pass_weights))
+    stream = []
+    for h in range(halves):
+        stream += [pass_copy(h, j) for j in range(parts[h])]
+        stream += [near_copy(h, k) for k in range(len(own_weights[h]))]
+    for copy in stream[:ahead]:
+        copy.start()
 
     def zero(ref, h, c):
         ref[h, :, c:c + TILE, :] = jnp.zeros((ref.shape[1], TILE, LANES), jnp.float32)
@@ -246,12 +251,12 @@
     @pl.when(has_above)
     def _():
         arrived(C.at[0], cond_recv.at[0])
-        arrived(C.at[3], cond_recv.at[3])
+        corner_wait(3)
 
     @pl.when(has_below)
     def _():
         arrived(C.at[1], cond_recv.at[1])
-        arrived(C.at[4], cond_recv.at[4])
+        corner_wait(4)
 
     @pl.when(jnp.logical_not(has_above))
     def _():
@@ -278,6 +283,8 @@
         d = 2 << r
         pl.semaphore_wait(hello.at[r], (me >= d).astype(jnp.int32) + (me + d < n).astype(jnp.int32))
 
+    for copy in stream[ahead:]:
+        copy.start()
     greet(0)
 
     first = lax.broadcasted_iota(jnp.int32, (2 * rows, LANES), 0) < rows
@@ -321,7 +328,7 @@
 
     TH[0:TILE, :] = jnp.zeros((TILE, LANES), jnp.float32)
     H[:, 0:TILE, :] = jnp.zeros((H.shape[0], TILE, LANES), jnp.float32)
-    lax.fori_loop(1, width // TILE - 1, edges, 0, unroll=2)
+    lax.fori_loop(1, width // TILE - 1, edges, 0, unroll=6)
 
     def spread(t, _):
         c = pl.multiple_of(t * TILE, TILE)
@@ -341,29 +348,25 @@
     tiles = width // TILE
 
     def relay(h, j):
-        arrived(X.at[h, pl.ds((1 - odd) * 2 * rows + 1, rows - 2), span(shared_at, j), :],
-                shared_recv.at[h, j])
+        arrived(X.at[h, pl.ds((1 - odd) * (2 * rows + 1), rows - 1), span(pass_at[h], j), :],
+                pass_recv.at[pass_sem[h] + j])
 
         @pl.when(can_relay)
         def _():
             relay_copy(h, j).start()
 
-    parts = len(shared_weights)
-    splits = cuts(tiles - 2, [1] * parts)
-    for j in range(parts):
+    splits = cuts(tiles - 2, [1] * parts[0])
+    for j in range(parts[0]):
         lax.fori_loop(1 + splits[j], 1 + splits[j + 1], spread, 0)
         relay(0, j)
         if j < rounds:
             greeted(j)
             if j + 1 < rounds:
                 greet(j + 1)
-    for r in range(parts, rounds):
-        greeted(r)
-        if r + 1 < rounds:
-            greet(r + 1)
-
-    def ends(h, lag, first, end):
-        return [first] + [PAD // TILE + core + bound - lag for bound in own_at[h][1:-1]] + [end]
+    for j in range(parts[0], rounds):
+        greeted(j)
+        if j + 1 < rounds:
+            greet(j + 1)
 
     def shape_of(cells, h, top):
         base = (chip * rows + top) * total_cols + core * cols - PAD
@@ -430,11 +433,29 @@
                 acc = tuple(s + term for s, term in zip(acc, terms))
             return acc
 
-        r_ends, w_ends, u_ends = (
-            ends(h, lag, 1 + (lag == 3), tiles - 1 - (lag == 3)) for lag in (1, 2, 3))
-        lax.fori_loop(r_ends[j], r_ends[j + 1], pass_r, 0)
-        lax.fori_loop(w_ends[j], w_ends[j + 1], pass_w, 0)
-        return lax.fori_loop(u_ends[j], u_ends[j + 1], pass_u, acc)
+        def sweep(lag, step, carry):
+            bounds = own_at[h]
+            begin, end = (1, tiles - 1) if lag < 3 else (2, tiles - 2)
+            offset = PAD // TILE - lag
+            final = j == len(bounds) - 2
+            start = begin if j == 0 else offset + core + bounds[j]
+            count = (end - 1 if final else offset + bounds[j + 1]) - (begin if j == 0 else offset + bounds[j])
+            extra = core if j == 0 else 1 - core if final else None
+            pairs = count // 2
+
+            def pair(i, carry):
+                return step(start + 2 * i + 1, step(start + 2 * i, carry))
+
+            carry = lax.fori_loop(0, pairs, pair, carry)
+            if count % 2:
+                carry = step(start + 2 * pairs, carry)
+            if extra is not None and not (j == 0 and final):
+                carry = lax.fori_loop(start + count, start + count + extra, step, carry)
+            return carry
+
+        sweep(1, pass_r, 0)
+        sweep(2, pass_w, 0)
+        return sweep(3, pass_u, acc)
 
     def sum_copy(h, d):
         return remote(S.at[h, me], S.at[h, me], sum_send.at[0], sum_recv.at[h], (me + d) % n)
@@ -489,26 +510,22 @@
         acc = zeros()
         relayed = 0
         for k in range(len(own_weights[h])):
-            while relayed < parts and shared_at[relayed] < own_at[h][k + 1]:
+            while relayed < parts[h] and pass_at[h][relayed] < own_at[h][k + 1]:
                 @pl.when(gets_relay)
                 def _():
-                    arrived(X.at[h, pl.ds(odd * 2 * rows + 1, rows - 2), span(shared_at, relayed), :],
-                            relay_recv.at[h, relayed])
+                    arrived(X.at[h, far_rows, span(pass_at[h], relayed), :], relay_recv.at[pass_sem[h] + relayed])
                 relayed += 1
 
-            @pl.when(has_diagonal)
-            def _():
-                arrived(X.at[h, odd * 2 * rows + (1 - odd) * (rows - 1), span(own_at[h], k), :],
-                        far_recv.at[h, k])
             arrived(X.at[h, (1 - odd) * 2 * rows + odd * (rows - 1), span(own_at[h], k), :],
-                    near_recv.at[h, k])
+                    near_recv.at[own_sem[h] + k])
             acc = compute(h, k, acc)
         send_sums(h, acc)
         if h < halves - 1:
-            for j in range(parts):
+            for j in range(parts[h + 1]):
                 relay(h + 1, j)
-                if j == parts // 2 - 1:
-                    finish(h)
+
+    for h in range(halves - 1):
+        finish(h)
 
     p, q = totals(halves - 1)
     coef_ref[...] = jnp.concatenate([p, q, jnp.zeros((TILE - 2, LANES), jnp.float32)], 0)
@@ -517,24 +534,27 @@
 
     @pl.when(has_above)
     def _():
-        drained(C.at[pl.ds(0, 2)], cond_send.at[1])
+        drained(C.at[0], cond_send.at[1])
+        drained(C.at[0, :, pl.ds(0, LANES)], cond_send.at[3])
 
     @pl.when(has_below)
     def _():
-        drained(C.at[pl.ds(0, 2)], cond_send.at[2])
+        drained(C.at[0], cond_send.at[2])
+        drained(C.at[0, :, pl.ds(0, LANES)], cond_send.at[4])
 
     drained(X.at[:, pl.ds(0, rows), pl.ds(0, TILE), :], side_send.at[0])
     drained(X.at[:, pl.ds(0, rows - 1), pl.ds(0, TILE), :], cross_send.at[0])
-    drained(X.at[:, pl.ds(0, rows - 1), pl.ds(0, cols), :], near_send.at[0])
+    drained(X.at[:, pl.ds(0, rows - 1), pl.ds(0, TILE), :], edge_send.at[0])
+    drained(X.at[:, pl.ds(0, rows), pl.ds(0, cols - TILE), :], near_send.at[0])
 
     @pl.when(has_diagonal)
     def _():
         drained(X.at[:, pl.ds(0, rows - 1), pl.ds(0, TILE), :], cross_send.at[1])
-        drained(X.at[:, pl.ds(0, 1), pl.ds(0, cols + (rows - 2) * TILE), :], far_send.at[0])
+        drained(X.at[:, pl.ds(0, rows - 1), pl.ds(0, TILE), :], far_send.at[0])
 
     @pl.when(can_relay)
     def _():
-        drained(X.at[:, pl.ds(0, rows - 2), pl.ds(0, cols - TILE), :], relay_send.at[0])
+        drained(X.at[:, pl.ds(0, rows - 1), pl.ds(0, cols - TILE), :], relay_send.at[0])
 
     drained(S.at[:, pl.ds(0, n - 1)], sum_send.at[0])
 
@@ -594,11 +614,11 @@
         drops = jax.ShapeDtypeStruct((halves, LANES), f32)
         vmem = pl.BlockSpec(memory_space=pltpu.VMEM)
         hbm = pl.BlockSpec(memory_space=pltpu.HBM)
-        shared_weights = (16, 16, 16, 15)
-        own_weights = ((16, 16, 16, 15),) * (halves - 1) + ((9, 9, 9, 9, 9, 8, 6, 4),)
-        parts, most = len(shared_weights), max(map(len, own_weights))
+        pass_weights = ((16, 16, 16, 15),) * (halves - 1) + ((12, 12, 12, 12, 8, 7),)
+        own_weights = ((32, 31),) * (halves - 1) + ((9, 9, 9, 9, 9, 8, 6, 4),)
+        passes, owns = sum(map(len, pass_weights)), sum(map(len, own_weights))
         stages = pl.pallas_call(
-            functools.partial(kernel, n, rows, cols, rounds, shared_weights, own_weights),
+            functools.partial(kernel, n, rows, cols, rounds, 3, pass_weights, own_weights),
             out_shape=(part, part, jax.ShapeDtypeStruct((4, rows, cols, LANES), f32),
                        jax.ShapeDtypeStruct((TILE, LANES), f32), drops),
             in_specs=[hbm] * 5,
@@ -622,10 +642,9 @@
                 pltpu.VMEM((halves, LANES), jnp.int32),
                 dma((4,)), dma((halves,)),
                 dma((5,)), dma((halves,)), dma((halves, 2)), dma((halves, 2)),
-                dma((halves, parts)), dma((halves, parts)),
-                dma((halves, most)), dma((halves, most)),
-                dma((halves,)), dma((3,)), dma((1,)), dma((2,)),
-                dma((1,)), dma((1,)), dma((1,)), dma((1,)),
+                dma((passes,)), dma((passes,)), dma((owns,)),
+                dma((halves,)), dma((5,)), dma((1,)), dma((2,)),
+                dma((1,)), dma((1,)), dma((1,)), dma((1,)), dma((1,)),
                 pltpu.SemaphoreType.REGULAR((rounds,)),
             ],
             compiler_params=pltpu.CompilerParams(

time: 95.4 us -> 61.8 us (0.65)
  Pallas kernels: 94.6 us -> 61 us
    pallas_call x1, Pallas kernels: 92.6 us -> 59 us  [shards(): pl.pallas_call(functools.partial(kernel, n, rows, cols, rounds, 3, pass_w...]
where the time goes in v1:
time: 61.8 us; the launch traced here: 61.7 us
  Pallas kernels  61 us (99%)
  between operations  0.64 us (1%)
    pallas_call x1, Pallas kernels, shards(): pl.pallas_call(functools.partial(kernel, n, rows, cols, rounds, 3, pass_w...  59 us
    pallas_call x1, Pallas kernels, shards(): pl.pallas_call(closing, out_shape=(field, field, drops), in_specs=[vmem]...  2.03 us

profile of v1, /device:TPU:0, one launch (start us, length us, event | category | flops | bytes accessed | tf_op | source)
XLA Modules:
  0.0 61.7 jit_solution(369580359071850108)
XLA Ops:
  0.6 59.0 %shard_map.76 = (f32[1,4,512,128]{3,2,1,0:T(8,128)S(1)}, f32[1,4,512,128]{3,2,1,0:T(8,128)S(1)}, f32[4,4,512,128]{3,2,1,0:T(8,128)S(1)}, f32[8,128]{1,0:T(8,128)S(1)}, f32[2,128]{1,0:T(2,128)S(1)}) custom-call(f32[16]{0:T(128)} %table_hbm.1, s32[1,4,512]{2,1,0:T(4,128)} %habitat_hbm.1, s32[2,128]{1,0:T(2,128)} %bitcast.3, s32[2,128]{1,0:T(2,128)} %bitcast.4, ...), custom_call_target="tpu_custom_call" | custom-call | tf_op jit(solution)/shard_map/pallas_call | solution.py:620
  59.6 2.0 %shard_map.77 = (f32[1,4,512,256]{3,2,1,0:T(8,128)}, f32[1,4,512,256]{3,2,1,0:T(8,128)}, f32[2,128]{1,0:T(2,128)}) custom-call(f32[1,4,512,128]{3,2,1,0:T(8,128)S(1)} %get-tuple-element.11.pot_ref, f32[1,4,512,128]{3,2,1,0:T(8,128)S(1)} %get-tuple-element.12.res_ref, f32[4,4,512,128]{3,2,1,0:T(8,128)S(1)} %get-tuple-element.13.field_ref, ...), custom_call_target="tpu_custom_call" | custom-call | tf_op jit(solution)/shard_map/pallas_call | solution.py:655

commit v2 on v1

--- a/solution.py
+++ b/solution.py
@@ -21,13 +21,13 @@
     return bounds
 
 
-def kernel(n, rows, cols, rounds, ahead, pass_weights, own_weights,
+def kernel(n, rows, cols, rounds, pass_weights, own_weights,
            table_hbm, habitat_hbm, source_hbm, ground_hbm, start_ref,
            pot_ref, res_ref, field_ref, coef_ref, drop_ref,
            X, R, W, U, V, H, D, C, T, TV, TH, S,
            table_ref, habitat_ref, source_ref, ground_ref, small_sem, load_sem,
-           cond_recv, side_recv, edge_recv, cross_recv, pass_recv, relay_recv, near_recv,
-           sum_recv, cond_send, side_send, cross_send, near_send, edge_send, far_send, relay_send, sum_send, hello):
+           cond_recv, side_recv, edge_recv, cross_recv, pass_recv, relay_recv, third_recv, help_recv, far_recv, near_recv,
+           sum_recv, cond_send, side_send, cross_send, near_send, edge_send, far_send, relay_send, pass_send, third_send, onward_send, forward_send, sum_send, hello):
     halves = X.shape[0]
     width = cols + 2 * PAD
     me = lax.axis_index("tile")
@@ -95,6 +95,10 @@
     def _():
         signal(barrier, relay_from)
 
+    @pl.when(can_relay)
+    def _():
+        signal(barrier, relay_to)
+
     for h in range(halves):
         load(h).start()
     for copy in smalls:
@@ -138,17 +142,52 @@
     def cross_wait(h, k):
         arrived(X.at[h, (near_rows, far_rows)[k], halo_at, :], cross_recv.at[h, k])
 
+    rank = jnp.where(odd == 0, chip // 2, chips // 2 - 1 - chip // 2)
+    pairs, tally = chips // 2, halves * body
+
+    def detours(k, h, j):
+        return (pairs - k) * 2 * tally > pairs * (2 * h * body + pass_at[h][j] + pass_at[h][j + 1])
+
+    def can_detour(h, j):
+        return pairs > 1 and detours(1, h, j)
+
+    outward = rows + odd * (rows - 1)
+    lent = odd * (3 * rows - 1)
+    guest = (1 - odd) * (3 * rows - 1)
+    far_row = odd * 2 * rows + (1 - odd) * (rows - 1)
+    far_there = (1 - odd) * 2 * rows + odd * (rows - 1)
+
     def pass_copy(h, j):
         at = span(pass_at[h], j)
-        return remote(X.at[h, pl.ds(rows + odd, rows - 1), at, :],
-                      X.at[h, pl.ds(odd * 2 * rows + odd, rows - 1), at, :],
-                      near_send.at[0], pass_recv.at[pass_sem[h] + j], partner)
+        return remote(X.at[h, pl.ds(rows + 1, rows - 2), at, :],
+                      X.at[h, pl.ds(odd * 2 * rows + 1, rows - 2), at, :],
+                      pass_send.at[0], pass_recv.at[pass_sem[h] + j], partner)
 
     def relay_copy(h, j):
         at = span(pass_at[h], j)
-        return remote(X.at[h, pl.ds((1 - odd) * (2 * rows + 1), rows - 1), at, :],
-                      X.at[h, far_rows, at, :],
+        return remote(X.at[h, pl.ds((1 - odd) * 2 * rows + 1, rows - 2), at, :],
+                      X.at[h, pl.ds(odd * 2 * rows + 1, rows - 2), at, :],
                       relay_send.at[0], relay_recv.at[pass_sem[h] + j], relay_to)
+
+    def third_copy(h, j):
+        at = span(pass_at[h], j)
+        return remote(X.at[h, outward, at, :], X.at[h, odd * (3 * rows - 1), at, :],
+                      third_send.at[0], third_recv.at[pass_sem[h] + j], partner)
+
+    def help_copy(h, j):
+        at = span(pass_at[h], j)
+        return remote(X.at[h, outward, at, :], X.at[h, lent, at, :],
+                      third_send.at[0], help_recv.at[pass_sem[h] + j], relay_from)
+
+    def onward_copy(h, j):
+        at = span(pass_at[h], j)
+        return remote(X.at[h, guest, at, :], X.at[h, far_row, at, :],
+                      onward_send.at[pass_sem[h] + j], far_recv.at[pass_sem[h] + j], relay_to)
+
+    def forward_copy(h, j):
+        at = span(pass_at[h], j)
+        return remote(X.at[h, lent, at, :], X.at[h, far_there, at, :],
+                      forward_send.at[pass_sem[h] + j], far_recv.at[pass_sem[h] + j], partner)
 
     def near_copy(h, k):
         at = span(own_at[h], k)
@@ -167,7 +206,8 @@
 
     pl.semaphore_wait(
         barrier,
-        1 + 2 * has_above.astype(jnp.int32) + 2 * has_below.astype(jnp.int32) + can_relay.astype(jnp.int32))
+        1 + 2 * has_above.astype(jnp.int32) + 2 * has_below.astype(jnp.int32)
+        + can_relay.astype(jnp.int32) + gets_relay.astype(jnp.int32))
 
     def cond_copy(target, slot, kind):
         return remote(C.at[5], C.at[slot], cond_send.at[kind], cond_recv.at[slot], target)
@@ -204,12 +244,28 @@
             edge_far(h).start()
 
     parts = list(map(len, pass_weights))
-    stream = []
+
     for h in range(halves):
-        stream += [pass_copy(h, j) for j in range(parts[h])]
-        stream += [near_copy(h, k) for k in range(len(own_weights[h]))]
-    for copy in stream[:ahead]:
-        copy.start()
+        for j in range(parts[h]):
+            if can_detour(h, j):
+                @pl.when(gets_relay & detours(rank, h, j))
+                def _():
+                    help_copy(h, j).start()
+
+    def send_pass(h, j):
+        pass_copy(h, j).start()
+
+        @pl.when(gets_relay & jnp.logical_not(detours(rank, h, j)))
+        def _():
+            third_copy(h, j).start()
+
+    def send_rest(h, done):
+        for j in range(done, parts[h]):
+            send_pass(h, j)
+        for k in range(len(own_weights[h])):
+            near_copy(h, k).start()
+
+    send_pass(0, 0)
 
     def zero(ref, h, c):
         ref[h, :, c:c + TILE, :] = jnp.zeros((ref.shape[1], TILE, LANES), jnp.float32)
@@ -230,11 +286,11 @@
 
         @pl.when(jnp.logical_not(has_above))
         def _():
-            X[h, 0:rows] = jnp.zeros((rows, width, LANES), jnp.float32)
+            X[h, 1:rows] = jnp.zeros((rows - 1, width, LANES), jnp.float32)
 
         @pl.when(jnp.logical_not(has_below))
         def _():
-            X[h, 2 * rows:3 * rows] = jnp.zeros((rows, width, LANES), jnp.float32)
+            X[h, 2 * rows:3 * rows - 1] = jnp.zeros((rows - 1, width, LANES), jnp.float32)
 
     for h in range(halves):
         arrived(X.at[h, near_rows, inner_at, :], edge_recv.at[h, 0])
@@ -283,8 +339,7 @@
         d = 2 << r
         pl.semaphore_wait(hello.at[r], (me >= d).astype(jnp.int32) + (me + d < n).astype(jnp.int32))
 
-    for copy in stream[ahead:]:
-        copy.start()
+    send_rest(0, 1)
     greet(0)
 
     first = lax.broadcasted_iota(jnp.int32, (2 * rows, LANES), 0) < rows
@@ -348,25 +403,50 @@
     tiles = width // TILE
 
     def relay(h, j):
-        arrived(X.at[h, pl.ds((1 - odd) * (2 * rows + 1), rows - 1), span(pass_at[h], j), :],
+        arrived(X.at[h, pl.ds((1 - odd) * 2 * rows + 1, rows - 2), span(pass_at[h], j), :],
                 pass_recv.at[pass_sem[h] + j])
 
         @pl.when(can_relay)
         def _():
             relay_copy(h, j).start()
 
-    splits = cuts(tiles - 2, [1] * parts[0])
-    for j in range(parts[0]):
-        lax.fori_loop(1 + splits[j], 1 + splits[j + 1], spread, 0)
-        relay(0, j)
-        if j < rounds:
-            greeted(j)
-            if j + 1 < rounds:
-                greet(j + 1)
-    for j in range(parts[0], rounds):
-        greeted(j)
-        if j + 1 < rounds:
-            greet(j + 1)
+    def onward(h, j):
+        @pl.when(can_relay & jnp.logical_not(detours(pairs - 1 - rank, h, j)))
+        def _():
+            arrived(X.at[h, guest, span(pass_at[h], j), :], third_recv.at[pass_sem[h] + j])
+            onward_copy(h, j).start()
+
+    def forward(h, j):
+        if can_detour(h, j):
+            @pl.when(can_relay & detours(rank + 1, h, j))
+            def _():
+                arrived(X.at[h, lent, span(pass_at[h], j), :], help_recv.at[pass_sem[h] + j])
+                forward_copy(h, j).start()
+
+    def meet(r):
+        if r < rounds:
+            greeted(r)
+            if r + 1 < rounds:
+                greet(r + 1)
+
+    steps = [[lambda j=j: relay(0, j), lambda j=j: onward(0, j)] for j in range(parts[0])]
+    steps = sum(steps, [])
+    lends = [(h, j) for h in range(halves) for j in range(parts[h])]
+    splits = cuts(tiles - 2, [1] * len(steps))
+    for i, step in enumerate(steps):
+        lax.fori_loop(1 + splits[i], 1 + splits[i + 1], spread, 0)
+        step()
+        meet(i)
+        if i == 0:
+            for j in range(parts[0]):
+                forward(0, j)
+        if i == 1:
+            for h, j in lends[parts[0]:]:
+                forward(h, j)
+            for h in range(1, halves):
+                send_rest(h, 0)
+    for r in range(len(steps), rounds):
+        meet(r)
 
     def shape_of(cells, h, top):
         base = (chip * rows + top) * total_cols + core * cols - PAD
@@ -513,7 +593,10 @@
             while relayed < parts[h] and pass_at[h][relayed] < own_at[h][k + 1]:
                 @pl.when(gets_relay)
                 def _():
-                    arrived(X.at[h, far_rows, span(pass_at[h], relayed), :], relay_recv.at[pass_sem[h] + relayed])
+                    arrived(X.at[h, pl.ds(odd * 2 * rows + 1, rows - 2), span(pass_at[h], relayed), :],
+                            relay_recv.at[pass_sem[h] + relayed])
+                    arrived(X.at[h, far_row, span(pass_at[h], relayed), :],
+                            far_recv.at[pass_sem[h] + relayed])
                 relayed += 1
 
             arrived(X.at[h, (1 - odd) * 2 * rows + odd * (rows - 1), span(own_at[h], k), :],
@@ -523,6 +606,7 @@
         if h < halves - 1:
             for j in range(parts[h + 1]):
                 relay(h + 1, j)
+                onward(h + 1, j)
 
     for h in range(halves - 1):
         finish(h)
@@ -545,7 +629,8 @@
     drained(X.at[:, pl.ds(0, rows), pl.ds(0, TILE), :], side_send.at[0])
     drained(X.at[:, pl.ds(0, rows - 1), pl.ds(0, TILE), :], cross_send.at[0])
     drained(X.at[:, pl.ds(0, rows - 1), pl.ds(0, TILE), :], edge_send.at[0])
-    drained(X.at[:, pl.ds(0, rows), pl.ds(0, cols - TILE), :], near_send.at[0])
+    drained(X.at[:, pl.ds(0, 1), pl.ds(0, cols - TILE), :], near_send.at[0])
+    drained(X.at[:, pl.ds(0, rows - 2), pl.ds(0, cols - TILE), :], pass_send.at[0])
 
     @pl.when(has_diagonal)
     def _():
@@ -554,7 +639,21 @@
 
     @pl.when(can_relay)
     def _():
-        drained(X.at[:, pl.ds(0, rows - 1), pl.ds(0, cols - TILE), :], relay_send.at[0])
+        drained(X.at[:, pl.ds(0, rows - 2), pl.ds(0, cols - TILE), :], relay_send.at[0])
+
+    @pl.when(gets_relay)
+    def _():
+        drained(X.at[:, pl.ds(0, 1), pl.ds(0, cols - TILE), :], third_send.at[0])
+
+    for h, j in lends:
+        @pl.when(can_relay & jnp.logical_not(detours(pairs - 1 - rank, h, j)))
+        def _():
+            drained(X.at[h, guest, span(pass_at[h], j), :], onward_send.at[pass_sem[h] + j])
+
+        if can_detour(h, j):
+            @pl.when(can_relay & detours(rank + 1, h, j))
+            def _():
+                drained(X.at[h, lent, span(pass_at[h], j), :], forward_send.at[pass_sem[h] + j])
 
     drained(S.at[:, pl.ds(0, n - 1)], sum_send.at[0])
 
@@ -614,11 +713,11 @@
         drops = jax.ShapeDtypeStruct((halves, LANES), f32)
         vmem = pl.BlockSpec(memory_space=pltpu.VMEM)
         hbm = pl.BlockSpec(memory_space=pltpu.HBM)
-        pass_weights = ((16, 16, 16, 15),) * (halves - 1) + ((12, 12, 12, 12, 8, 7),)
+        pass_weights = ((32, 31),) * (halves - 1) + ((13, 13, 13, 12, 12),)
         own_weights = ((32, 31),) * (halves - 1) + ((9, 9, 9, 9, 9, 8, 6, 4),)
         passes, owns = sum(map(len, pass_weights)), sum(map(len, own_weights))
         stages = pl.pallas_call(
-            functools.partial(kernel, n, rows, cols, rounds, 3, pass_weights, own_weights),
+            functools.partial(kernel, n, rows, cols, rounds, pass_weights, own_weights),
             out_shape=(part, part, jax.ShapeDtypeStruct((4, rows, cols, LANES), f32),
                        jax.ShapeDtypeStruct((TILE, LANES), f32), drops),
             in_specs=[hbm] * 5,
@@ -642,9 +741,10 @@
                 pltpu.VMEM((halves, LANES), jnp.int32),
                 dma((4,)), dma((halves,)),
                 dma((5,)), dma((halves,)), dma((halves, 2)), dma((halves, 2)),
-                dma((passes,)), dma((passes,)), dma((owns,)),
+                dma((passes,)), dma((passes,)), dma((passes,)), dma((passes,)), dma((passes,)), dma((owns,)),
                 dma((halves,)), dma((5,)), dma((1,)), dma((2,)),
-                dma((1,)), dma((1,)), dma((1,)), dma((1,)), dma((1,)),
+                dma((1,)), dma((1,)), dma((1,)), dma((1,)), dma((1,)), dma((1,)),
+                dma((passes,)), dma((passes,)), dma((1,)),
                 pltpu.SemaphoreType.REGULAR((rounds,)),
             ],
             compiler_params=pltpu.CompilerParams(

time: 61.8 us -> 60.4 us (0.977)
  Pallas kernels: 61 us -> 59.6 us
    pallas_call x1, Pallas kernels: 59 us -> 57.6 us  [shards(): pl.pallas_call(functools.partial(kernel, n, rows, cols, rounds, pass_weig...]
where the time goes in v2:
time: 60.4 us; the launch traced here: 60.3 us
  Pallas kernels  59.6 us (99%)
  between operations  0.64 us (1%)
    pallas_call x1, Pallas kernels, shards(): pl.pallas_call(functools.partial(kernel, n, rows, cols, rounds, pass_weig...  57.6 us
    pallas_call x1, Pallas kernels, shards(): pl.pallas_call(closing, out_shape=(field, field, drops), in_specs=[vmem]...  2.03 us

profile of v2, /device:TPU:0, one launch (start us, length us, event | category | flops | bytes accessed | tf_op | source)
XLA Modules:
  0.0 60.3 jit_solution(2509793404466178968)
XLA Ops:
  0.6 57.6 %shard_map.76 = (f32[1,4,512,128]{3,2,1,0:T(8,128)S(1)}, f32[1,4,512,128]{3,2,1,0:T(8,128)S(1)}, f32[4,4,512,128]{3,2,1,0:T(8,128)S(1)}, f32[8,128]{1,0:T(8,128)S(1)}, f32[2,128]{1,0:T(2,128)S(1)}) custom-call(f32[16]{0:T(128)} %table_hbm.1, s32[1,4,512]{2,1,0:T(4,128)} %habitat_hbm.1, s32[2,128]{1,0:T(2,128)} %bitcast.3, s32[2,128]{1,0:T(2,128)} %bitcast.4, ...), custom_call_target="tpu_custom_call" | custom-call | tf_op jit(solution)/shard_map/pallas_call | solution.py:719
  58.2 2.0 %shard_map.77 = (f32[1,4,512,256]{3,2,1,0:T(8,128)}, f32[1,4,512,256]{3,2,1,0:T(8,128)}, f32[2,128]{1,0:T(2,128)}) custom-call(f32[1,4,512,128]{3,2,1,0:T(8,128)S(1)} %get-tuple-element.11.pot_ref, f32[1,4,512,128]{3,2,1,0:T(8,128)S(1)} %get-tuple-element.12.res_ref, f32[4,4,512,128]{3,2,1,0:T(8,128)S(1)} %get-tuple-element.13.field_ref, ...), custom_call_target="tpu_custom_call" | custom-call | tf_op jit(solution)/shard_map/pallas_call | solution.py:755

commit v3 on v2

--- a/solution.py
+++ b/solution.py
@@ -259,12 +259,6 @@
         def _():
             third_copy(h, j).start()
 
-    def send_rest(h, done):
-        for j in range(done, parts[h]):
-            send_pass(h, j)
-        for k in range(len(own_weights[h])):
-            near_copy(h, k).start()
-
     send_pass(0, 0)
 
     def zero(ref, h, c):
@@ -339,7 +333,9 @@
         d = 2 << r
         pl.semaphore_wait(hello.at[r], (me >= d).astype(jnp.int32) + (me + d < n).astype(jnp.int32))
 
-    send_rest(0, 1)
+    for j in range(1, parts[0]):
+        send_pass(0, j)
+    near_copy(0, 0).start()
     greet(0)
 
     first = lax.broadcasted_iota(jnp.int32, (2 * rows, LANES), 0) < rows
@@ -444,7 +440,11 @@
             for h, j in lends[parts[0]:]:
                 forward(h, j)
             for h in range(1, halves):
-                send_rest(h, 0)
+                for j in range(parts[h]):
+                    send_pass(h, j)
+            for h in range(halves):
+                for k in range(h == 0, len(own_weights[h])):
+                    near_copy(h, k).start()
     for r in range(len(steps), rounds):
         meet(r)
 
@@ -587,26 +587,33 @@
         def _():
             cross_wait(h, 1)
 
-        acc = zeros()
-        relayed = 0
-        for k in range(len(own_weights[h])):
-            while relayed < parts[h] and pass_at[h][relayed] < own_at[h][k + 1]:
-                @pl.when(gets_relay)
-                def _():
-                    arrived(X.at[h, pl.ds(odd * 2 * rows + 1, rows - 2), span(pass_at[h], relayed), :],
-                            relay_recv.at[pass_sem[h] + relayed])
-                    arrived(X.at[h, far_row, span(pass_at[h], relayed), :],
-                            far_recv.at[pass_sem[h] + relayed])
-                relayed += 1
-
-            arrived(X.at[h, (1 - odd) * 2 * rows + odd * (rows - 1), span(own_at[h], k), :],
-                    near_recv.at[own_sem[h] + k])
-            acc = compute(h, k, acc)
-        send_sums(h, acc)
-        if h < halves - 1:
-            for j in range(parts[h + 1]):
-                relay(h + 1, j)
-                onward(h + 1, j)
+    sums = [zeros() for _ in range(halves)]
+    relayed = [0] * halves
+
+    def advance(h, k):
+        while relayed[h] < parts[h] and pass_at[h][relayed[h]] < own_at[h][k + 1]:
+            j = relayed[h]
+
+            @pl.when(gets_relay)
+            def _():
+                arrived(X.at[h, pl.ds(odd * 2 * rows + 1, rows - 2), span(pass_at[h], j), :],
+                        relay_recv.at[pass_sem[h] + j])
+                arrived(X.at[h, far_row, span(pass_at[h], j), :], far_recv.at[pass_sem[h] + j])
+            relayed[h] += 1
+
+        arrived(X.at[h, (1 - odd) * 2 * rows + odd * (rows - 1), span(own_at[h], k), :],
+                near_recv.at[own_sem[h] + k])
+        sums[h] = compute(h, k, sums[h])
+
+    advance(0, 0)
+    for h in range(1, halves):
+        for j in range(parts[h]):
+            relay(h, j)
+            onward(h, j)
+    for h in range(halves):
+        for k in range(h == 0, len(own_weights[h])):
+            advance(h, k)
+        send_sums(h, sums[h])
 
     for h in range(halves - 1):
         finish(h)
@@ -713,8 +720,8 @@
         drops = jax.ShapeDtypeStruct((halves, LANES), f32)
         vmem = pl.BlockSpec(memory_space=pltpu.VMEM)
         hbm = pl.BlockSpec(memory_space=pltpu.HBM)
-        pass_weights = ((32, 31),) * (halves - 1) + ((13, 13, 13, 12, 12),)
-        own_weights = ((32, 31),) * (halves - 1) + ((9, 9, 9, 9, 9, 8, 6, 4),)
+        pass_weights = ((32, 31),) * (halves - 1) + ((14, 14, 14, 12, 9),)
+        own_weights = ((48, 15),) * (halves - 1) + ((9, 9, 9, 9, 9, 8, 6, 4),)
         passes, owns = sum(map(len, pass_weights)), sum(map(len, own_weights))
         stages = pl.pallas_call(
             functools.partial(kernel, n, rows, cols, rounds, pass_weights, own_weights),

time: 60.4 us -> 59.2 us (0.980)
  Pallas kernels: 59.6 us -> 58.4 us
    pallas_call x1, Pallas kernels: 57.6 us -> 56.4 us  [shards(): pl.pallas_call(functools.partial(kernel, n, rows, cols, rounds, pass_weig...]
where the time goes in v3:
time: 59.2 us; the launch traced here: 59 us
  Pallas kernels  58.4 us (99%)
  between operations  0.64 us (1%)
    pallas_call x1, Pallas kernels, shards(): pl.pallas_call(functools.partial(kernel, n, rows, cols, rounds, pass_weig...  56.4 us
    pallas_call x1, Pallas kernels, shards(): pl.pallas_call(closing, out_shape=(field, field, drops), in_specs=[vmem]...  2.03 us

profile of v3, /device:TPU:0, one launch (start us, length us, event | category | flops | bytes accessed | tf_op | source)
XLA Modules:
  0.0 59.0 jit_solution(10269766035533218460)
XLA Ops:
  0.6 56.4 %shard_map.76 = (f32[1,4,512,128]{3,2,1,0:T(8,128)S(1)}, f32[1,4,512,128]{3,2,1,0:T(8,128)S(1)}, f32[4,4,512,128]{3,2,1,0:T(8,128)S(1)}, f32[8,128]{1,0:T(8,128)S(1)}, f32[2,128]{1,0:T(2,128)S(1)}) custom-call(f32[16]{0:T(128)} %table_hbm.1, s32[1,4,512]{2,1,0:T(4,128)} %habitat_hbm.1, s32[2,128]{1,0:T(2,128)} %bitcast.3, s32[2,128]{1,0:T(2,128)} %bitcast.4, ...), custom_call_target="tpu_custom_call" | custom-call | tf_op jit(solution)/shard_map/pallas_call | solution.py:726
  57.0 2.0 %shard_map.77 = (f32[1,4,512,256]{3,2,1,0:T(8,128)}, f32[1,4,512,256]{3,2,1,0:T(8,128)}, f32[2,128]{1,0:T(2,128)}) custom-call(f32[1,4,512,128]{3,2,1,0:T(8,128)S(1)} %get-tuple-element.11.pot_ref, f32[1,4,512,128]{3,2,1,0:T(8,128)S(1)} %get-tuple-element.12.res_ref, f32[4,4,512,128]{3,2,1,0:T(8,128)S(1)} %get-tuple-element.13.field_ref, ...), custom_call_target="tpu_custom_call" | custom-call | tf_op jit(solution)/shard_map/pallas_call | solution.py:762

commit v4 on v3

--- a/solution.py
+++ b/solution.py
@@ -26,7 +26,7 @@
            pot_ref, res_ref, field_ref, coef_ref, drop_ref,
            X, R, W, U, V, H, D, C, T, TV, TH, S,
            table_ref, habitat_ref, source_ref, ground_ref, small_sem, load_sem,
-           cond_recv, side_recv, edge_recv, cross_recv, pass_recv, relay_recv, third_recv, help_recv, far_recv, near_recv,
+           cond_recv, side_recv, edge_recv, cross_recv, pass_recv, relay_recv, third_recv, help_recv, near_recv,
            sum_recv, cond_send, side_send, cross_send, near_send, edge_send, far_send, relay_send, pass_send, third_send, onward_send, forward_send, sum_send, hello):
     halves = X.shape[0]
     width = cols + 2 * PAD
@@ -78,6 +78,11 @@
             (source_hbm, source_ref), (ground_hbm, ground_ref)))
     ]
 
+    for copy in smalls:
+        copy.start()
+    for h in range(halves):
+        load(h).start()
+
     barrier = pltpu.get_barrier_semaphore()
     signal(barrier, side)
 
@@ -99,10 +104,6 @@
     def _():
         signal(barrier, relay_to)
 
-    for h in range(halves):
-        load(h).start()
-    for copy in smalls:
-        copy.start()
 
     inner = pl.multiple_of(PAD + (1 - core) * (cols - TILE), TILE)
     outer = pl.multiple_of((1 - core) * TILE + core * (PAD + cols), TILE)
@@ -182,12 +183,12 @@
     def onward_copy(h, j):
         at = span(pass_at[h], j)
         return remote(X.at[h, guest, at, :], X.at[h, far_row, at, :],
-                      onward_send.at[pass_sem[h] + j], far_recv.at[pass_sem[h] + j], relay_to)
+                      onward_send.at[pass_sem[h] + j], relay_recv.at[pass_sem[h] + j], relay_to)
 
     def forward_copy(h, j):
         at = span(pass_at[h], j)
         return remote(X.at[h, lent, at, :], X.at[h, far_there, at, :],
-                      forward_send.at[pass_sem[h] + j], far_recv.at[pass_sem[h] + j], partner)
+                      forward_send.at[pass_sem[h] + j], relay_recv.at[pass_sem[h] + j], partner)
 
     def near_copy(h, k):
         at = span(own_at[h], k)
@@ -335,7 +336,9 @@
 
     for j in range(1, parts[0]):
         send_pass(0, j)
-    near_copy(0, 0).start()
+    early = len(own_weights[0]) - 1
+    for k in range(early):
+        near_copy(0, k).start()
     greet(0)
 
     first = lax.broadcasted_iota(jnp.int32, (2 * rows, LANES), 0) < rows
@@ -443,7 +446,7 @@
                 for j in range(parts[h]):
                     send_pass(h, j)
             for h in range(halves):
-                for k in range(h == 0, len(own_weights[h])):
+                for k in range(0 if h else early, len(own_weights[h])):
                     near_copy(h, k).start()
     for r in range(len(steps), rounds):
         meet(r)
@@ -473,7 +476,7 @@
             mid = after
 
     def zeros():
-        return tuple(jnp.zeros((TILE, LANES), jnp.float32) for _ in range(7))
+        return tuple(jnp.zeros((TILE, LANES), jnp.float32) for _ in range(10))
 
     def compute(h, j, acc):
         def named(cells, top, count):
@@ -487,7 +490,7 @@
         def pass_r(t, _):
             c = pl.multiple_of(t * TILE, TILE)
             for k, a, _mid, _g, column in applied(X, h, 1, count_r, c, 0, gnd_r):
-                R[h, k, pl.ds(c, TILE), :] = jnp.where(column == src_r[k], 1.0 - a, -a)
+                R[h, k, pl.ds(c, TILE), :] = jnp.where(column == src_r[k], 1.0, 0.0) - a
             return 0
 
         def pass_w(t, _):
@@ -508,9 +511,11 @@
                 else:
                     for place, value in enumerate((x, r, w, u)):
                         field_ref[place, k, to, :] = value
-                sign = jnp.where(column == src_u[k], 1.0, 0.0) - jnp.where(grounded, 1.0, 0.0)
-                terms = (r * r, r * w, w * w, w * u, sign * x, sign * r, sign * w)
-                acc = tuple(s + term for s, term in zip(acc, terms))
+                terms = (r * r, r * w, w * w, w * u)
+                sourced = column == src_u[k]
+                acc = tuple(s + term for s, term in zip(acc, terms)) + tuple(
+                    jnp.where(sourced, value, s) for s, value in zip(acc[4:7], (x, r, w))) + tuple(
+                    jnp.where(grounded, value, s) for s, value in zip(acc[7:], (x, r, w)))
             return acc
 
         def sweep(lag, step, carry):
@@ -541,7 +546,8 @@
         return remote(S.at[h, me], S.at[h, me], sum_send.at[0], sum_recv.at[h], (me + d) % n)
 
     def send_sums(h, acc):
-        sums = [jnp.sum(s, axis=0, keepdims=True) for s in acc]
+        ends = tuple(at_source - at_ground for at_source, at_ground in zip(acc[4:7], acc[7:]))
+        sums = [jnp.sum(s, axis=0, keepdims=True) for s in acc[:4] + ends]
         S[h, me] = jnp.concatenate(sums + [jnp.zeros((1, LANES), jnp.float32)], 0)
         lax.fori_loop(1, n, lambda d, _: (sum_copy(h, d).start(), 0)[1], 0)
 
@@ -596,22 +602,21 @@
 
             @pl.when(gets_relay)
             def _():
-                arrived(X.at[h, pl.ds(odd * 2 * rows + 1, rows - 2), span(pass_at[h], j), :],
-                        relay_recv.at[pass_sem[h] + j])
-                arrived(X.at[h, far_row, span(pass_at[h], j), :], far_recv.at[pass_sem[h] + j])
+                arrived(X.at[h, far_rows, span(pass_at[h], j), :], relay_recv.at[pass_sem[h] + j])
             relayed[h] += 1
 
         arrived(X.at[h, (1 - odd) * 2 * rows + odd * (rows - 1), span(own_at[h], k), :],
                 near_recv.at[own_sem[h] + k])
         sums[h] = compute(h, k, sums[h])
 
-    advance(0, 0)
+    for k in range(early):
+        advance(0, k)
     for h in range(1, halves):
         for j in range(parts[h]):
             relay(h, j)
             onward(h, j)
     for h in range(halves):
-        for k in range(h == 0, len(own_weights[h])):
+        for k in range(0 if h else early, len(own_weights[h])):
             advance(h, k)
         send_sums(h, sums[h])
 
@@ -721,7 +726,7 @@
         vmem = pl.BlockSpec(memory_space=pltpu.VMEM)
         hbm = pl.BlockSpec(memory_space=pltpu.HBM)
         pass_weights = ((32, 31),) * (halves - 1) + ((14, 14, 14, 12, 9),)
-        own_weights = ((48, 15),) * (halves - 1) + ((9, 9, 9, 9, 9, 8, 6, 4),)
+        own_weights = ((32, 20, 11),) * (halves - 1) + ((11, 11, 11, 11, 8, 7, 4),)
         passes, owns = sum(map(len, pass_weights)), sum(map(len, own_weights))
         stages = pl.pallas_call(
             functools.partial(kernel, n, rows, cols, rounds, pass_weights, own_weights),
@@ -748,7 +753,7 @@
                 pltpu.VMEM((halves, LANES), jnp.int32),
                 dma((4,)), dma((halves,)),
                 dma((5,)), dma((halves,)), dma((halves, 2)), dma((halves, 2)),
-                dma((passes,)), dma((passes,)), dma((passes,)), dma((passes,)), dma((passes,)), dma((owns,)),
+                dma((passes,)), dma((passes,)), dma((passes,)), dma((passes,)), dma((owns,)),
                 dma((halves,)), dma((5,)), dma((1,)), dma((2,)),
                 dma((1,)), dma((1,)), dma((1,)), dma((1,)), dma((1,)), dma((1,)),
                 dma((passes,)), dma((passes,)), dma((1,)),

time: 59.2 us -> 59 us (level)
  no operation moved by 1% of the time
where the time goes in v4:
time: 59 us; the launch traced here: 58.8 us
  Pallas kernels  58.2 us (99%)
  between operations  0.64 us (1%)
    pallas_call x1, Pallas kernels, shards(): pl.pallas_call(functools.partial(kernel, n, rows, cols, rounds, pass_weig...  56.2 us
    pallas_call x1, Pallas kernels, shards(): pl.pallas_call(closing, out_shape=(field, field, drops), in_specs=[vmem]...  2.03 us

profile of v4, /device:TPU:0, one launch (start us, length us, event | category | flops | bytes accessed | tf_op | source)
XLA Modules:
  0.0 58.8 jit_solution(8567293301236606434)
XLA Ops:
  0.6 56.2 %shard_map.76 = (f32[1,4,512,128]{3,2,1,0:T(8,128)S(1)}, f32[1,4,512,128]{3,2,1,0:T(8,128)S(1)}, f32[4,4,512,128]{3,2,1,0:T(8,128)S(1)}, f32[8,128]{1,0:T(8,128)S(1)}, f32[2,128]{1,0:T(2,128)S(1)}) custom-call(f32[16]{0:T(128)} %table_hbm.1, s32[1,4,512]{2,1,0:T(4,128)} %habitat_hbm.1, s32[2,128]{1,0:T(2,128)} %bitcast.3, s32[2,128]{1,0:T(2,128)} %bitcast.4, ...), custom_call_target="tpu_custom_call" | custom-call | tf_op jit(solution)/shard_map/pallas_call | solution.py:731
  56.8 2.0 %shard_map.77 = (f32[1,4,512,256]{3,2,1,0:T(8,128)}, f32[1,4,512,256]{3,2,1,0:T(8,128)}, f32[2,128]{1,0:T(2,128)}) custom-call(f32[1,4,512,128]{3,2,1,0:T(8,128)S(1)} %get-tuple-element.11.pot_ref, f32[1,4,512,128]{3,2,1,0:T(8,128)S(1)} %get-tuple-element.12.res_ref, f32[4,4,512,128]{3,2,1,0:T(8,128)S(1)} %get-tuple-element.13.field_ref, ...), custom_call_target="tpu_custom_call" | custom-call | tf_op jit(solution)/shard_map/pallas_call | solution.py:767

commit v5 on v4

--- a/solution.py
+++ b/solution.py
@@ -204,6 +204,8 @@
         cond = jnp.where(cells == level, table_ref[level], cond)
     C[5, 0:rows, :] = cond
     C[5, rows:2 * rows, :] = cond
+    for slot in (0, 1):
+        C[slot, rows:2 * rows, :] = jnp.zeros_like(cond)
 
     pl.semaphore_wait(
         barrier,
@@ -213,6 +215,10 @@
     def cond_copy(target, slot, kind):
         return remote(C.at[5], C.at[slot], cond_send.at[kind], cond_recv.at[slot], target)
 
+    def rows_copy(target, slot, kind):
+        return remote(C.at[5, pl.ds(0, rows), :], C.at[slot, pl.ds(0, rows), :],
+                      cond_send.at[kind], cond_recv.at[slot], target)
+
     def inner_lanes(which):
         return pl.ds(pl.multiple_of(which * (cols - LANES), LANES), LANES)
 
@@ -227,12 +233,12 @@
 
     @pl.when(has_above)
     def _():
-        cond_copy(me - 2, 1, 1).start()
+        rows_copy(me - 2, 1, 1).start()
         corner_copy(side - 2, 4, 3).start()
 
     @pl.when(has_below)
     def _():
-        cond_copy(me + 2, 0, 2).start()
+        rows_copy(me + 2, 0, 2).start()
         corner_copy(side + 2, 3, 4).start()
 
     for h in range(halves):
@@ -301,12 +307,12 @@
 
     @pl.when(has_above)
     def _():
-        arrived(C.at[0], cond_recv.at[0])
+        arrived(C.at[0, pl.ds(0, rows), :], cond_recv.at[0])
         corner_wait(3)
 
     @pl.when(has_below)
     def _():
-        arrived(C.at[1], cond_recv.at[1])
+        arrived(C.at[1, pl.ds(0, rows), :], cond_recv.at[1])
         corner_wait(4)
 
     @pl.when(jnp.logical_not(has_above))
@@ -630,12 +636,12 @@
 
     @pl.when(has_above)
     def _():
-        drained(C.at[0], cond_send.at[1])
+        drained(C.at[0, pl.ds(0, rows), :], cond_send.at[1])
         drained(C.at[0, :, pl.ds(0, LANES)], cond_send.at[3])
 
     @pl.when(has_below)
     def _():
-        drained(C.at[0], cond_send.at[2])
+        drained(C.at[0, pl.ds(0, rows), :], cond_send.at[2])
         drained(C.at[0, :, pl.ds(0, LANES)], cond_send.at[4])
 
     drained(X.at[:, pl.ds(0, rows), pl.ds(0, TILE), :], side_send.at[0])

time: 59 us -> 58.7 us (level)
  no operation moved by 1% of the time
where the time goes in v5:
time: 58.7 us; the launch traced here: 58.5 us
  Pallas kernels  57.9 us (99%)
  between operations  0.64 us (1%)
    pallas_call x1, Pallas kernels, shards(): pl.pallas_call(functools.partial(kernel, n, rows, cols, rounds, pass_weig...  55.9 us
    pallas_call x1, Pallas kernels, shards(): pl.pallas_call(closing, out_shape=(field, field, drops), in_specs=[vmem]...  2.03 us

profile of v5, /device:TPU:0, one launch (start us, length us, event | category | flops | bytes accessed | tf_op | source)
XLA Modules:
  0.0 58.5 jit_solution(6386724337921007759)
XLA Ops:
  0.6 55.9 %shard_map.76 = (f32[1,4,512,128]{3,2,1,0:T(8,128)S(1)}, f32[1,4,512,128]{3,2,1,0:T(8,128)S(1)}, f32[4,4,512,128]{3,2,1,0:T(8,128)S(1)}, f32[8,128]{1,0:T(8,128)S(1)}, f32[2,128]{1,0:T(2,128)S(1)}) custom-call(f32[16]{0:T(128)} %table_hbm.1, s32[1,4,512]{2,1,0:T(4,128)} %habitat_hbm.1, s32[2,128]{1,0:T(2,128)} %bitcast.3, s32[2,128]{1,0:T(2,128)} %bitcast.4, ...), custom_call_target="tpu_custom_call" | custom-call | tf_op jit(solution)/shard_map/pallas_call | solution.py:737
  56.5 2.0 %shard_map.77 = (f32[1,4,512,256]{3,2,1,0:T(8,128)}, f32[1,4,512,256]{3,2,1,0:T(8,128)}, f32[2,128]{1,0:T(2,128)}) custom-call(f32[1,4,512,128]{3,2,1,0:T(8,128)S(1)} %get-tuple-element.11.pot_ref, f32[1,4,512,128]{3,2,1,0:T(8,128)S(1)} %get-tuple-element.12.res_ref, f32[4,4,512,128]{3,2,1,0:T(8,128)S(1)} %get-tuple-element.13.field_ref, ...), custom_call_target="tpu_custom_call" | custom-call | tf_op jit(solution)/shard_map/pallas_call | solution.py:773
